TPU v7x, 32 devices: a whole 2x2x4 slice. The times are simulated.
32 devices in a mesh: groups: 2 (over y), rows: 4 (over z), cols: 2 (over x), sub: 2 (over core).
Axes of the slice: x: 2, y: 2, z: 4, core: 2. Of those that a mesh axis runs over, the one named last changes fastest.
Arguments:
- stored_vectors: bfloat16 [3072, 8192], P(('cols', 'sub'), ('groups', 'rows')), parts along dimension 1, may hold values from -0.59765625 to 0.59765625
- previous_columns: bfloat16 [8192, 256], P(('groups', 'rows', 'cols', 'sub')), parts along dimension 0, may hold values from -3 to 3
- pivots: int32 [512], P('groups'), parts along dimension 0, may hold values from 0 to 4095, as said below
- diagonal: float32 [8192], P(('groups', 'rows', 'cols', 'sub')), parts along dimension 0, may hold values from 2 to 32
- ket_blocks: bfloat16 [128, 128, 256], P(('groups', 'rows', 'cols', 'sub')), parts along dimension 0, may hold values from -6 to 6
- shell_tags: int32 [128, 128], P(('groups', 'rows', 'cols', 'sub')), parts along dimension 0, may hold values from 0 to 3
- target_blocks: int32 [32, 4], P('groups'), parts along dimension 0, may hold values from 0 to 31, as said below
- block_counts: int32 [32], P('groups'), parts along dimension 0, may hold values from 0 to 4, as said below
- shell_norms: float32 [4], replicated, may hold values from 0.5 to 2
Outputs:
- new_vectors: bfloat16 [8192, 256], P(('groups', 'rows', 'cols', 'sub')), parts along dimension 0
- diag_out: float32 [8192], P(('groups', 'rows', 'cols', 'sub')), parts along dimension 0
- next_columns: bfloat16 [8192, 256], P(('groups', 'rows', 'cols', 'sub')), parts along dimension 0
There are 2 independent parts, one for each index of `groups`. A program takes and returns all parts, laid end to end along the dimension named above; an argument that names none is the same for every part. Nothing has to cross between parts.
Inputs may be any that keep to these rules, and one draw needn't show every extreme that they name: `pivots`: 256 distinct AO pairs. `target_blocks`: the used slots of all owners name every block of the 32 blocks exactly once; a used slot's block lies on a device with the owner's cols and sub indices (blocks g * 2 to g * 2 + 1 lie on the device of linear index g, rows slowest; owner o is the device of linear index o). At most 1 of one owner's used slots go to one device, and some owner reaches that in every draw. Entries of unused slots are arbitrary blocks. `block_counts`: some owner uses all 4 slots in every draw.
All inputs are finite; a program needn't handle non-finite values.
Results may differ from a plain program's by a relative error of at most 0.0004.
Values may be sent and summed in bfloat16 or wider, within the bound.
A program may use at most 64 MiB of HBM per device.

v0:
```python
import jax
import jax.numpy as jnp
from jax import lax
from jax.sharding import PartitionSpec as P


def slot_plan(row_targets, count, column_size, per_device):
    slot_count = row_targets.shape[0]
    slots = jnp.arange(slot_count, dtype=jnp.int32)
    valid = slots < count
    receiver = row_targets // (column_size * per_device)
    within = row_targets % per_device
    earlier = (
        (receiver[:, None] == receiver[None, :])
        & valid[:, None]
        & valid[None, :]
        & (slots[None, :] < slots[:, None])
    )
    ranking = jnp.sum(earlier.astype(jnp.int32), axis=1)
    return (valid, receiver, ranking, within)


def body(
    stored_vectors,
    previous_columns,
    pivots,
    diagonal,
    ket_blocks,
    shell_tags,
    target_blocks,
    block_counts,
    shell_norms,
):
    rows_here = previous_columns.shape[0]
    batch = previous_columns.shape[1]
    block_rows = ket_blocks.shape[1]
    slot_count = ket_blocks.shape[0]
    per_device = rows_here // block_rows
    band_rows = stored_vectors.shape[1]
    band_index = lax.axis_index("rows")
    device_index = lax.axis_index(("rows", "cols", "sub"))
    column_index = lax.axis_index(("cols", "sub"))
    column_size = lax.axis_size(("cols", "sub"))
    band_size = lax.axis_size("rows")
    peer_slots = (slot_count + band_size - 1) // band_size
    local_pivots = pivots - device_index * rows_here
    matches = jnp.arange(rows_here, dtype=jnp.int32)[:, None] == local_pivots[None, :]
    diag_terms = jnp.sum(jnp.where(matches, diagonal[:, None], jnp.float32(0.0)), axis=0)
    pivot_diag = lax.psum(diag_terms, ("rows", "cols", "sub"))
    band_pivots = pivots - band_index * band_rows
    inside = (band_pivots >= 0) & (band_pivots < band_rows)
    clamped = jnp.clip(band_pivots, 0, band_rows - 1)
    taken = jnp.take(stored_vectors, clamped, axis=1).astype(jnp.float32)
    picked = jnp.where(inside[None, :], taken, jnp.float32(0.0))
    pivot_rows = lax.psum(picked, "rows").astype(jnp.bfloat16)
    kinds = jnp.arange(shell_norms.shape[0], dtype=jnp.int32)
    factor = jnp.sum(
        jnp.where(shell_tags[..., None] == kinds, shell_norms, jnp.float32(0.0)), axis=-1
    )
    fresh = (ket_blocks.astype(jnp.float32) * factor[..., None]).astype(jnp.bfloat16)
    own_targets = lax.dynamic_index_in_dim(target_blocks, device_index, 0, keepdims=False)
    own_count = lax.dynamic_index_in_dim(block_counts, device_index, 0, keepdims=False)
    valid, receiver, ranking, within = slot_plan(own_targets, own_count, column_size, per_device)
    lines = jnp.arange(band_size * peer_slots, dtype=jnp.int32)[:, None]
    routing = (
        (lines // peer_slots == receiver[None, :])
        & (lines % peer_slots == ranking[None, :])
        & valid[None, :]
    ).astype(jnp.bfloat16)
    outgoing = jnp.dot(
        routing, fresh.reshape(slot_count, block_rows * batch), preferred_element_type=jnp.float32
    )
    outgoing = outgoing.astype(jnp.bfloat16).reshape(band_size, peer_slots, block_rows, batch)
    incoming = lax.all_to_all(outgoing, "rows", split_axis=0, concat_axis=0, tiled=True)
    sources = jnp.arange(band_size, dtype=jnp.int32) * column_size + column_index
    source_targets = jnp.take(target_blocks, sources, axis=0)
    source_counts = jnp.take(block_counts, sources, axis=0)
    plan_each = jax.vmap(
        lambda row_targets, count: slot_plan(row_targets, count, column_size, per_device)
    )
    source_valid, source_receiver, source_rank, source_within = plan_each(
        source_targets, source_counts
    )
    arriving = source_valid & (source_receiver == band_index)
    places = jnp.arange(per_device, dtype=jnp.int32)[:, None, None, None]
    peer_lines = jnp.arange(peer_slots, dtype=jnp.int32)[None, None, :, None]
    hits = (
        (source_within[None, :, None, :] == places)
        & (source_rank[None, :, None, :] == peer_lines)
        & arriving[None, :, None, :]
    )
    placement = (
        jnp.any(hits, axis=3).astype(jnp.bfloat16).reshape(per_device, band_size * peer_slots)
    )
    arranged = jnp.dot(
        placement,
        incoming.reshape(band_size * peer_slots, block_rows * batch),
        preferred_element_type=jnp.float32,
    )
    next_columns = arranged.astype(jnp.bfloat16).reshape(rows_here, batch)
    product = lax.psum_scatter(
        lax.dot_general(
            stored_vectors, pivot_rows, (((0,), (0,)), ((), ())), preferred_element_type=jnp.float32
        ),
        ("cols", "sub"),
        scatter_dimension=0,
        tiled=True,
    )
    residual_cols = previous_columns.astype(jnp.float32) - product
    scaled = residual_cols / jnp.sqrt(pivot_diag)[None, :]
    new_vectors = scaled.astype(jnp.bfloat16)
    diag_out = diagonal - jnp.sum(scaled * scaled, axis=1)
    return (new_vectors, diag_out, next_columns)


def solution(mesh):
    return jax.shard_map(
        body,
        mesh=mesh,
        in_specs=(
            P(("cols", "sub"), ("groups", "rows")),
            P(("groups", "rows", "cols", "sub"), None),
            P("groups"),
            P(("groups", "rows", "cols", "sub")),
            P(("groups", "rows", "cols", "sub"), None, None),
            P(("groups", "rows", "cols", "sub"), None),
            P("groups", None),
            P("groups"),
            P(),
        ),
        out_specs=(
            P(("groups", "rows", "cols", "sub"), None),
            P(("groups", "rows", "cols", "sub")),
            P(("groups", "rows", "cols", "sub"), None),
        ),
        check_vma=False,
    )
```

profile of v0, /device:TPU:0, one launch (start us, length us, event | category | flops | bytes accessed | tf_op | source)
XLA Modules:
  0.0 100.1 jit_solution(16816415105481037228)
XLA Ops:
  7.2 1.7 %copy.26 = bf16[768,1024]{0,1:T(8,128)(2,1)S(1)} copy(bf16[768,1024]{1,0:T(8,128)(2,1)} %param.9) | data formatting | bytes 3145728 | tf_op args[0]
  9.0 1.2 %gather_fusion = bf16[256,768]{1,0:T(8,128)(2,1)S(1)} fusion(bf16[768,1024]{0,1:T(8,128)(2,1)S(1)} %copy.26, s32[1024]{0:T(1024)S(1)} %pad_clamp_fusion.1), kind=kCustom, calls=%fused_computation | custom fusion | bytes 787456 | tf_op jit(solution)/shard_map/jit(_take)/gather | solution.py:53
  10.2 0.2 select_bitcast_fusion
  10.4 37.4 %all-reduce.1 = bf16[768,256]{0,1:T(8,128)(2,1)S(1)} all-reduce(f32[768,256]{0,1:T(8,128)S(1)} %select_bitcast_fusion), channel_id=1, replica_groups=mesh['groups'=2,'rows'=4,'cols'=2,'sub'=2] {'rows'}, use_global_device_ids=true, to_apply=%region_0.1 | all-reduce | flops 196608 | bytes 1179648 | tf_op jit(solution)/shard_map/psum | solution.py:55
  47.9 1.6 %convolution_bitcast_fusion = f32[1024,256]{0,1:T(8,128)} fusion(bf16[768,1024]{1,0:T(8,128)(2,1)S(1)} %copy-done.1, bf16[768,256]{0,1:T(8,128)(2,1)S(1)} %all-reduce.1), kind=kOutput, calls=%fused_computation.5 | convolution fusion | flops 402653184 | bytes 3014656 | tf_op jit(solution)/shard_map/dot_general | solution.py:102
  49.5 0.1 select_reduce_fusion.1
  49.6 0.1 fusion.1
  49.7 0.2 copy.30
  50.0 0.2 copy-done.4
  50.1 0.2 dynamic-slice_reduce_fusion
  50.3 0.6 dynamic_slice.9
  50.9 0.6 iota_compare_fusion.6
  51.6 0.2 convert_reduce_fusion.1
  51.8 0.3 convolution_convert_fusion
  52.1 0.7 copy.34
  52.8 3.4 %all-to-all-start = ((bf16[4,1,128,256]{3,2,1,0:T(8,128)(2,1)}), bf16[4,1,128,256]{3,2,1,0:T(8,128)(2,1)S(1)}, u32[]{:S(2)}, u32[]{:S(2)}) async-start(bf16[4,1,128,256]{3,2,1,0:T(8,128)(2,1)} %bitcast.26), calls=%async_computation.1 | async-start | bytes 524288 | tf_op jit(solution)/shard_map/all_to_all | solution.py:74
  56.2 0.1 copy.27
  56.3 0.6 gather_fusion.2
  57.0 0.6 gather_fusion.1
  57.6 0.1 compare_and_fusion
  57.6 0.2 convert_reduce_fusion
  57.9 0.1 select_reduce_fusion
  58.0 31.2 %psum.15 = f32[256]{0:T(256)S(1)} all-reduce(f32[256]{0:T(256)S(1)} %select_reduce_fusion), channel_id=1, replica_groups=mesh['groups'=2,'rows'=4,'cols'=2,'sub'=2] {'rows','cols','sub'}, use_global_device_ids=true, to_apply=%region_3.4 | all-reduce | flops 256 | bytes 2048 | tf_op jit(solution)/shard_map/psum | solution.py:49
  89.2 0.1 copy.25
  89.3 0.1 add_select_fusion.2
  89.4 0.2 fusion.4
  89.6 0.2 copy.32
  89.8 0.3 convolution_convert_fusion.1
  90.1 0.7 reshape.328
  90.8 1.1 %multiply_reduce_fusion = (f32[256]{0:T(256)S(1)}, bf16[256,256]{0,1:T(8,128)(2,1)S(1)}) fusion(f32[256]{0:T(256)S(1)} %sqrt.3, f32[256,256]{0,1:T(8,128)} %reduce-scatter.2.cloned.1.call-done, bf16[256,256]{0,1:T(8,128)(2,1)S(1)} %copy.25), kind=kLoop, calls=%fused_computation.11 | loop fusion | flops 392960 | bytes 526336 | tf_op jit(solution)/shard_map/reduce_sum | solution.py:112
  91.9 0.8 copy.29
  92.6 0.6 sub.35
  (32 shorter events, 0.2 us)
Async XLA Ops:
  7.2 83.6 %reduce-scatter.2.cloned.1.call-start = ((), (), s32[]{:S(2)}) async-start(), calls=%async_computation.2 | async-start | bytes 1310720 | tf_op jit(solution)/shard_map/reduce_scatter | solution.py:101
  7.2 1.7 %copy-start.6 = (s32[256]{0:T(256)S(1)}, s32[256]{0:T(256)}, u32[]{:S(2)}) copy-start(s32[256]{0:T(256)} %param.11) | copy-start | bytes 3076
  10.2 37.6 %copy-start.1 = (bf16[768,1024]{1,0:T(8,128)(2,1)S(1)}, bf16[768,1024]{1,0:T(8,128)(2,1)}, u32[]{:S(2)}) copy-start(bf16[768,1024]{1,0:T(8,128)(2,1)} %param.9) | copy-start | bytes 4718596
  47.8 1.6 %copy-start.7 = (s32[4,128]{1,0:T(4,128)S(1)}, s32[4,128]{1,0:T(4,128)}, u32[]{:S(2)}) copy-start(s32[4,128]{1,0:T(4,128)} %param.14) | copy-start | bytes 6148
  47.8 1.6 %copy-start.8 = (f32[4]{0:T(128)S(1)}, f32[4]{0:T(128)}, u32[]{:S(2)}) copy-start(f32[4]{0:T(128)} %param.17) | copy-start | bytes 52
  47.9 1.7 %copy-start.2 = (bf16[4,128,256]{2,1,0:T(8,128)(2,1)S(1)}, bf16[4,128,256]{2,1,0:T(8,128)(2,1)}, u32[]{:S(2)}) copy-start(bf16[4,128,256]{2,1,0:T(8,128)(2,1)} %param.13) | copy-start | bytes 786436
  49.4 0.7 copy-start.4
  49.4 0.9 copy-start
  49.6 8.3 %copy-start.5 = (f32[256]{0:T(256)S(1)}, f32[256]{0:T(256)}, u32[]{:S(2)}) copy-start(f32[256]{0:T(256)} %param.12) | copy-start | bytes 3076
  49.6 39.6 %copy-start.3 = (bf16[256,256]{1,0:T(8,128)(2,1)S(1)}, bf16[256,256]{1,0:T(8,128)(2,1)}, u32[]{:S(2)}) copy-start(bf16[256,256]{1,0:T(8,128)(2,1)} %param.10) | copy-start | bytes 393220
  52.8 36.7 %all-to-all-start = ((bf16[4,1,128,256]{3,2,1,0:T(8,128)(2,1)}), bf16[4,1,128,256]{3,2,1,0:T(8,128)(2,1)S(1)}, u32[]{:S(2)}, u32[]{:S(2)}) async-start(bf16[4,1,128,256]{3,2,1,0:T(8,128)(2,1)} %bitcast.26), calls=%async_computation.1 | async-start | bytes 524288 | tf_op jit(solution)/shard_map/all_to_all | solution.py:74
Sparse Core Ops, SparseCore 0:
  49.6 24.2 reduce-scatter.1
where the time goes:
time: 100 us
  blocking collectives  68.6 us (69%)
  between operations  14.3 us (14%)
  local copies, waits for them, and re-layouts  7.74 us (8%)
  other arithmetic  3.79 us (4%)
  starting transfers between devices  3.44 us (3%)
  matrix products  2.14 us (2%)
    psum x1, blocking collectives, body(): pivot_rows = lax.psum(picked, 'rows').astype(jnp.bfloat16)  37.4 us
    psum x1, blocking collectives, body(): pivot_diag = lax.psum(diag_terms, ('rows', 'cols', 'sub'))  31.2 us
    unnamed x25, local copies, waits for them, and re-layouts  4.02 us
    all_to_all x1, starting transfers between devices, body(): lax.all_to_all(outgoing, 'rows', split_axis=0, concat_axis=0, tiled=True)  3.4 us
  transfers between devices with their start and end apart: 2, of which 0 were waited for; matrix products, arithmetic and copies ran while one was open for 6% of the time, Pallas kernels for 0%

commit v1 on v0

--- a/solution.py
+++ b/solution.py
@@ -46,7 +46,8 @@
     local_pivots = pivots - device_index * rows_here
     matches = jnp.arange(rows_here, dtype=jnp.int32)[:, None] == local_pivots[None, :]
     diag_terms = jnp.sum(jnp.where(matches, diagonal[:, None], jnp.float32(0.0)), axis=0)
-    pivot_diag = lax.psum(diag_terms, ("rows", "cols", "sub"))
+    shards = lax.all_gather(diag_terms, ("rows", "cols", "sub"), axis=0, tiled=False)
+    pivot_diag = shards.sum(axis=0)
     band_pivots = pivots - band_index * band_rows
     inside = (band_pivots >= 0) & (band_pivots < band_rows)
     clamped = jnp.clip(band_pivots, 0, band_rows - 1)

time: 100 us -> 91.1 us (0.911)
  blocking collectives: 68.6 us -> 59.3 us
    psum x1 -> x0, blocking collectives: 31.2 us -> none  [body(): pivot_diag = lax.psum(diag_terms, ('rows', 'cols', 'sub'))]
    all_gather x0 -> x1, blocking collectives: none -> 21.8 us  [body(): lax.all_gather(diag_terms, ('rows', 'cols', 'sub'), axis=0, tiled=False)]
  transfers between devices with their start and end apart: 2 -> 2, of which waited for: 0 -> 0; matrix products, arithmetic and copies ran while one was open for 6% -> 7% of each run, Pallas kernels for 0% -> 0%
where the time goes in v1:
time: 91.1 us; the launch traced here: 90.7 us
  blocking collectives  59.3 us (65%)
  between operations  14.3 us (16%)
  local copies, waits for them, and re-layouts  7.74 us (8%)
  other arithmetic  3.83 us (4%)
  starting transfers between devices  3.44 us (4%)
  matrix products  2.14 us (2%)
    psum x1, blocking collectives, body(): pivot_rows = lax.psum(picked, 'rows').astype(jnp.bfloat16)  37.4 us
    all_gather x1, blocking collectives, body(): lax.all_gather(diag_terms, ('rows', 'cols', 'sub'), axis=0, tiled=False)  21.8 us
    unnamed x25, local copies, waits for them, and re-layouts  4.02 us
    all_to_all x1, starting transfers between devices, body(): lax.all_to_all(outgoing, 'rows', split_axis=0, concat_axis=0, tiled=True)  3.4 us
  transfers between devices with their start and end apart: 2, of which 0 were waited for; matrix products, arithmetic and copies ran while one was open for 7% of the time, Pallas kernels for 0%

profile of v1, /device:TPU:0, one launch (start us, length us, event | category | flops | bytes accessed | tf_op | source)
XLA Modules:
  0.0 90.7 jit_solution(16961252042723225403)
XLA Ops:
  7.2 1.7 %copy.26 = bf16[768,1024]{0,1:T(8,128)(2,1)S(1)} copy(bf16[768,1024]{1,0:T(8,128)(2,1)} %param.9) | data formatting | bytes 3145728 | tf_op args[0]
  9.0 1.2 %gather_fusion = bf16[256,768]{1,0:T(8,128)(2,1)S(1)} fusion(bf16[768,1024]{0,1:T(8,128)(2,1)S(1)} %copy.26, s32[1024]{0:T(1024)S(1)} %pad_clamp_fusion.1), kind=kCustom, calls=%fused_computation | custom fusion | bytes 787456 | tf_op jit(solution)/shard_map/jit(_take)/gather | solution.py:54
  10.2 0.2 select_bitcast_fusion
  10.4 37.4 %all-reduce.1 = bf16[768,256]{0,1:T(8,128)(2,1)S(1)} all-reduce(f32[768,256]{0,1:T(8,128)S(1)} %select_bitcast_fusion), channel_id=1, replica_groups=mesh['groups'=2,'rows'=4,'cols'=2,'sub'=2] {'rows'}, use_global_device_ids=true, to_apply=%region_0.1 | all-reduce | flops 196608 | bytes 1179648 | tf_op jit(solution)/shard_map/psum | solution.py:56
  47.9 1.6 %convolution_bitcast_fusion = f32[1024,256]{0,1:T(8,128)} fusion(bf16[768,1024]{1,0:T(8,128)(2,1)S(1)} %copy-done.1, bf16[768,256]{0,1:T(8,128)(2,1)S(1)} %all-reduce.1), kind=kOutput, calls=%fused_computation.5 | convolution fusion | flops 402653184 | bytes 3014656 | tf_op jit(solution)/shard_map/dot_general | solution.py:103
  49.5 0.1 select_reduce_fusion.1
  49.6 0.1 fusion.1
  49.7 0.2 copy.30
  50.0 0.2 copy-done.4
  50.1 0.2 dynamic-slice_reduce_fusion
  50.3 0.6 dynamic_slice.9
  50.9 0.6 iota_compare_fusion.6
  51.6 0.2 convert_reduce_fusion.1
  51.8 0.3 convolution_convert_fusion
  52.1 0.7 copy.34
  52.8 3.4 %all-to-all-start = ((bf16[4,1,128,256]{3,2,1,0:T(8,128)(2,1)}), bf16[4,1,128,256]{3,2,1,0:T(8,128)(2,1)S(1)}, u32[]{:S(2)}, u32[]{:S(2)}) async-start(bf16[4,1,128,256]{3,2,1,0:T(8,128)(2,1)} %bitcast.27), calls=%async_computation.1 | async-start | bytes 524288 | tf_op jit(solution)/shard_map/all_to_all | solution.py:75
  56.2 0.1 copy.27
  56.3 0.6 gather_fusion.2
  57.0 0.6 gather_fusion.1
  57.6 0.1 compare_and_fusion
  57.6 0.2 convert_reduce_fusion
  57.9 0.1 select_reduce_fusion
  58.0 21.8 %all-gather.1 = f32[16,1,256]{2,1,0:T(1,128)S(1)} all-gather(f32[1,1,256]{2,1,0:T(1,128)S(1)} %bitcast.32), channel_id=2, replica_groups=mesh['groups'=2,'rows'=4,'cols'=2,'sub'=2] {'rows','cols','sub'}, dimensions={0}, use_global_device_ids=true | all-gather | bytes 17408 | tf_op jit(solution)/shard_map/all_gather | solution.py:49
  79.9 0.1 copy.25
  80.0 0.1 add_select_fusion.2
  80.1 0.2 fusion.4
  80.2 0.2 copy.32
  80.5 0.3 convolution_convert_fusion.1
  80.7 0.7 reshape.330
  81.5 1.1 %multiply_reduce_fusion = (f32[256]{0:T(256)S(1)}, bf16[256,256]{0,1:T(8,128)(2,1)S(1)}) fusion(f32[256]{0:T(256)S(1)} %sqrt.7, f32[256,256]{0,1:T(8,128)} %reduce-scatter.2.cloned.1.call-done, bf16[256,256]{0,1:T(8,128)(2,1)S(1)} %copy.25), kind=kLoop, calls=%fused_computation.11 | loop fusion | flops 392960 | bytes 526336 | tf_op jit(solution)/shard_map/reduce_sum | solution.py:113
  82.6 0.8 copy.29
  83.3 0.6 sub.35
  (33 shorter events, 0.2 us)
Async XLA Ops:
  7.2 74.3 %reduce-scatter.2.cloned.1.call-start = ((), (), s32[]{:S(2)}) async-start(), calls=%async_computation.2 | async-start | bytes 1310720 | tf_op jit(solution)/shard_map/reduce_scatter | solution.py:102
  7.2 1.7 %copy-start.6 = (s32[256]{0:T(256)S(1)}, s32[256]{0:T(256)}, u32[]{:S(2)}) copy-start(s32[256]{0:T(256)} %param.11) | copy-start | bytes 3076
  10.2 37.6 %copy-start.1 = (bf16[768,1024]{1,0:T(8,128)(2,1)S(1)}, bf16[768,1024]{1,0:T(8,128)(2,1)}, u32[]{:S(2)}) copy-start(bf16[768,1024]{1,0:T(8,128)(2,1)} %param.9) | copy-start | bytes 4718596
  47.8 1.6 %copy-start.7 = (s32[4,128]{1,0:T(4,128)S(1)}, s32[4,128]{1,0:T(4,128)}, u32[]{:S(2)}) copy-start(s32[4,128]{1,0:T(4,128)} %param.14) | copy-start | bytes 6148
  47.8 1.6 %copy-start.8 = (f32[4]{0:T(128)S(1)}, f32[4]{0:T(128)}, u32[]{:S(2)}) copy-start(f32[4]{0:T(128)} %param.17) | copy-start | bytes 52
  47.9 1.7 %copy-start.2 = (bf16[4,128,256]{2,1,0:T(8,128)(2,1)S(1)}, bf16[4,128,256]{2,1,0:T(8,128)(2,1)}, u32[]{:S(2)}) copy-start(bf16[4,128,256]{2,1,0:T(8,128)(2,1)} %param.13) | copy-start | bytes 786436
  49.4 0.7 copy-start.4
  49.4 0.9 copy-start
  49.6 8.3 %copy-start.5 = (f32[256]{0:T(256)S(1)}, f32[256]{0:T(256)}, u32[]{:S(2)}) copy-start(f32[256]{0:T(256)} %param.12) | copy-start | bytes 3076
  49.6 30.3 %copy-start.3 = (bf16[256,256]{1,0:T(8,128)(2,1)S(1)}, bf16[256,256]{1,0:T(8,128)(2,1)}, u32[]{:S(2)}) copy-start(bf16[256,256]{1,0:T(8,128)(2,1)} %param.10) | copy-start | bytes 393220
  52.8 27.4 %all-to-all-start = ((bf16[4,1,128,256]{3,2,1,0:T(8,128)(2,1)}), bf16[4,1,128,256]{3,2,1,0:T(8,128)(2,1)S(1)}, u32[]{:S(2)}, u32[]{:S(2)}) async-start(bf16[4,1,128,256]{3,2,1,0:T(8,128)(2,1)} %bitcast.27), calls=%async_computation.1 | async-start | bytes 524288 | tf_op jit(solution)/shard_map/all_to_all | solution.py:75
Sparse Core Ops, SparseCore 0:
  49.6 24.1 reduce-scatter.1
